TPU v7x, 32 devices: a whole 2x2x4 slice. The times are simulated.
32 devices in a mesh: ctx: 8 (over y, x, core), tp: 4 (over z).
Axes of the slice: x: 2, y: 2, z: 4, core: 2. Of those that a mesh axis runs over, the one named last changes fastest.
Arguments:
- hidden_in: bfloat16 [2048, 4096], P(('ctx', 'tp')), may hold values from -6 to 6
- norm_gain: float32 [4096], replicated, may hold values from 0.5 to 1.5
- proj_weight: bfloat16 [4096, 4096], P(None, 'tp'), may hold values from -0.09375 to 0.09375
- conv_in: bfloat16 [2048, 4096], P('ctx', 'tp'), may hold values from -6 to 6
- conv_weight: float32 [4, 4096], P(None, 'tp'), may hold values from -3 to 3
- conv_bias: float32 [4096], P('tp'), may hold values from -3 to 3
- act_grad: bfloat16 [2048, 4096], P('ctx', 'tp'), may hold values from -6 to 6
Outputs:
- hidden_input_gradient: bfloat16 [2048, 4096], P(('ctx', 'tp'))
- norm_gain_gradient: float32 [4096], replicated
- taps_grad: float32 [4, 4096], P(None, 'tp')
- bias_grad: float32 [4096], P('tp')
All inputs are finite; a program needn't handle non-finite values.
Results may differ from a plain program's by a relative error of at most 0.013.
Values may be sent and summed in bfloat16 or wider, within the bound.
No kernel may reach another device: no remote copies, remote signals or barrier semaphores. Data moves between devices by JAX's collectives and lax.ppermute only.
A program may use at most 64 MiB of HBM per device.

v0:
```python
import jax
import jax.numpy as jnp
from jax import lax
from jax.sharding import PartitionSpec as P


def from_behind(block, axis, distance):
    devices = range(lax.axis_size(axis))
    route = [(i - distance, i) for i in devices if i - distance in devices]
    return lax.ppermute(block, axis, route)


def preact_of(padded, taps, offset, count_tok):
    tap_count = taps.shape[0]
    return offset[None, :] + sum(
        (
            taps[index][None, :] * padded[tap_count - 1 - index : tap_count - 1 - index + count_tok]
            for index in range(tap_count)
        )
    )


def grad_of(preact, cotangent):
    sigmoid_v = jax.nn.sigmoid(preact)
    return cotangent.astype(jnp.float32) * sigmoid_v * (1.0 + preact * (1.0 - sigmoid_v))


def on_device(hidden_in, norm_gain, proj_weight, conv_in, conv_weight, conv_bias, act_grad):
    count_tok = conv_in.shape[0]
    tap_count = conv_weight.shape[0]
    edge_rows = tap_count - 1
    earlier = from_behind(conv_in[count_tok - edge_rows :], "ctx", 1)
    later_in, later_grad = from_behind((conv_in[:edge_rows], act_grad[:edge_rows]), "ctx", -1)
    padded = jnp.concatenate([earlier, conv_in], 0).astype(jnp.float32)
    preact = preact_of(padded, conv_weight, conv_bias, count_tok)
    pre_grad = grad_of(preact, act_grad)
    tail_pad = jnp.concatenate([conv_in[count_tok - edge_rows :], later_in], 0).astype(jnp.float32)
    tail_pre = preact_of(tail_pad, conv_weight, conv_bias, edge_rows)
    next_grad = grad_of(tail_pre, later_grad)
    taps_part = jnp.stack(
        [
            jnp.sum(pre_grad * padded[edge_rows - index : edge_rows - index + count_tok], 0)
            for index in range(tap_count)
        ],
        0,
    )
    bias_part = jnp.sum(pre_grad, 0)
    taps_grad, bias_grad = lax.psum((taps_part, bias_part), "ctx")
    after = jnp.concatenate([pre_grad, next_grad], 0)
    in_grad = sum(
        (
            conv_weight[index][None, :] * after[index : index + count_tok]
            for index in range(tap_count)
        )
    ).astype(jnp.bfloat16)
    whole_term = lax.dot_general(
        in_grad, proj_weight, (((1,), (1,)), ((), ())), preferred_element_type=jnp.float32
    )
    normalized_gradient = lax.psum_scatter(
        whole_term.astype(jnp.bfloat16), "tp", scatter_dimension=0, tiled=True
    ).astype(jnp.float32)
    hidden_state = hidden_in.astype(jnp.float32)
    root_mean_square = jnp.sqrt(jnp.mean(hidden_state * hidden_state, -1, keepdims=True) + 1e-05)
    normalized_input = hidden_state / root_mean_square
    norm_gain_gradient = lax.psum(jnp.sum(normalized_gradient * normalized_input, 0), ("ctx", "tp"))
    scaled_gradient = norm_gain[None, :] * normalized_gradient
    mean_correction = jnp.mean(scaled_gradient * normalized_input, -1, keepdims=True)
    hidden_input_gradient = (
        (scaled_gradient - normalized_input * mean_correction) / root_mean_square
    ).astype(jnp.bfloat16)
    return (hidden_input_gradient, norm_gain_gradient, taps_grad, bias_grad)


def solution(mesh):
    return jax.shard_map(
        on_device,
        mesh=mesh,
        in_specs=(
            P(("ctx", "tp"), None),
            P(),
            P(None, "tp"),
            P("ctx", "tp"),
            P(None, "tp"),
            P("tp"),
            P("ctx", "tp"),
        ),
        out_specs=(P(("ctx", "tp"), None), P(), P(None, "tp"), P("tp")),
        check_vma=False,
    )
```

profile of v0, /device:TPU:0, one launch (start us, length us, event | category | flops | bytes accessed | tf_op | source)
XLA Modules:
  0.0 122.8 jit_solution(8762573390390648197)
XLA Ops:
  7.2 0.0 copy-start.2
  7.2 0.0 copy-start.4
  7.2 0.0 reduce-scatter.2.cloned.1.call-start
  7.2 0.8 fusion.26
  8.0 2.4 %collective-permute-start = (bf16[3,1024]{1,0:T(4,128)(2,1)S(1)}, bf16[3,1024]{1,0:T(4,128)(2,1)S(1)}, u32[]{:S(2)}, u32[]{:S(2)}) collective-permute-start(bf16[3,1024]{1,0:T(4,128)(2,1)S(1)} %get-tuple-element.14), channel_id=1, source_target_pairs={{0,4},{4,8},{8,12},{12,16},{16,20},{20,24},{24,28},{1,5},{5,9},{9,... | collective-permute-start | bytes 18440 | tf_op jit(solution)/shard_map/ppermute | solution.py:10
  10.4 1.3 %collective-permute-start.2 = (bf16[3,1024]{1,0:T(4,128)(2,1)S(1)}, bf16[3,1024]{1,0:T(4,128)(2,1)S(1)}, u32[]{:S(2)}, u32[]{:S(2)}) collective-permute-start(bf16[3,1024]{1,0:T(4,128)(2,1)S(1)} %get-tuple-element.15), channel_id=1, source_target_pairs={{4,0},{8,4},{12,8},{16,12},{20,16},{24,20},{28,24},{5,1},{9,5},{13... | collective-permute-start | bytes 18440 | tf_op jit(solution)/shard_map/ppermute | solution.py:10
  11.7 0.7 slice.76
  12.5 1.3 %collective-permute-start.1 = (bf16[3,1024]{1,0:T(4,128)(2,1)S(1)}, bf16[3,1024]{1,0:T(4,128)(2,1)S(1)}, u32[]{:S(2)}, u32[]{:S(2)}) collective-permute-start(bf16[3,1024]{1,0:T(4,128)(2,1)S(1)} %slice.76), channel_id=1, source_target_pairs={{4,0},{8,4},{12,8},{16,12},{20,16},{24,20},{28,24},{5,1},{9,5},{13... | collective-permute-start | bytes 18440 | tf_op jit(solution)/shard_map/ppermute | solution.py:10
  13.7 0.9 fusion.27
  14.6 0.0 collective-permute-done
  14.6 1.2 maximum_convert_fusion
  15.8 0.0 copy-done.2
  15.8 0.0 copy-done.4
  15.9 1.3 %multiply_reduce_fusion.3 = (f32[1024]{0:T(1024)S(1)}, f32[1024]{0:T(1024)S(1)}, f32[1024]{0:T(1024)S(1)}, f32[1024]{0:T(1024)S(1)}, f32[1024]{0:T(1024)S(1)}, /*index=5*/f32[256,1024]{1,0:T(8,128)S(1)}) fusion(f32[259,1024]{1,0:T(8,128)S(1)} %maximum_convert_fusion, f32[1024]{0:T(1024)S(1)} %bitcast.15, f32[1024]{0:T(1024)S(1)} %bitcast.18, ...), kind=kLoop, calls=%fused_computation.27 | loop fusion | flops 6810624 | bytes 5808128 | tf_op jit(solution)/shard_map/reduce_sum | solution.py:42
  17.1 0.0 collective-permute-done.2
  17.2 1.1 collective-permute-done.1
  18.3 7.4 %convolution_convert_fusion = bf16[256,4096]{1,0:T(8,128)(2,1)} fusion(bf16[4096,1024]{1,0:T(8,128)(2,1)} %param.9, f32[3,1024]{1,0:T(4,128)S(1)} %add_multiply_fusion.1, f32[256,1024]{1,0:T(8,128)S(1)} %get-tuple-element.13, f32[1024]{0:T(1024)S(1)} %bitcast.17, f32[1024]{0:T(1024)S(1)} %bitcast.20, f32[1024]{0:T(1024)S(1)} %bitcast.14, f32[1024]{0:T(1024)S(1)} %bitcast.11), kind=kOutput, calls=%fused_computation | convolution fusion | flops 2151415808 | bytes 11563008 | tf_op jit(solution)/shard_map/dot_general | solution.py:56
  25.6 0.0 copy-start
  25.6 0.0 copy-start.3
  25.6 0.0 reduce-scatter.2.cloned.1.call-update
  25.7 1.0 copy-done
  26.7 0.2 fusion.6
  26.9 29.4 %all-reduce = (f32[4,1024]{1,0:T(4,128)}, f32[1024]{0:T(1024)}) all-reduce(f32[4,1024]{1,0:T(4,128)S(1)} %pad_maximum_fusion.1, f32[1024]{0:T(1024)S(1)} %get-tuple-element.10), channel_id=1, replica_groups=mesh['ctx'=8,'tp'=4] {'ctx'}, use_global_device_ids=true, to_apply=%region_9.0 | all-reduce | flops 5120 | bytes 40960 | tf_op jit(solution)/shard_map/psum | solution.py:48
  56.4 17.4 %reduce-scatter.2.cloned.1.call-done = bf16[64,4096]{1,0:T(8,128)(2,1)} async-done(((bf16[256,4096]{1,0:T(8,128)(2,1)}), bf16[64,4096]{1,0:T(8,128)(2,1)}) %reduce-scatter.2.cloned.1.call-update) | async-done | bytes 524304 | tf_op jit(solution)/shard_map/reduce_scatter | solution.py:59
  73.7 0.0 copy-done.3
  73.7 0.0 copy-start.1
  73.7 1.6 %fusion.5 = (f32[4096]{0:T(1024)S(1)}, f32[64]{0:T(128)S(1)}) fusion(bf16[64,4096]{1,0:T(8,128)(2,1)} %reduce-scatter.2.cloned.1.call-done, f32[64]{0:T(128)S(1)} %add_sqrt_fusion, bf16[64,4096]{1,0:T(8,128)(2,1)S(1)} %copy-done, f32[4096]{0:T(1024)S(1)} %copy-done.3), kind=kLoop, calls=%fused_computation.12 | loop fusion | flops 2092992 | bytes 1081856 | tf_op jit(solution)/shard_map/reduce_sum | solution.py:65
  75.3 39.5 %psum.21 = f32[4096]{0:T(1024)} all-reduce(f32[4096]{0:T(1024)S(1)} %get-tuple-element.8), channel_id=1, replica_groups=mesh['ctx'=8,'tp'=4] {'ctx','tp'}, use_global_device_ids=true, to_apply=%region_4.0 | all-reduce | flops 4096 | bytes 32768 | tf_op jit(solution)/shard_map/psum | solution.py:65
  114.8 0.0 copy-done.1
  114.8 1.1 fusion.4
  (5 shorter events, 0.1 us)
Async XLA Ops:
  7.2 8.7 %copy-start.2 = (bf16[256,1024]{1,0:T(8,128)(2,1)S(1)}, bf16[256,1024]{1,0:T(8,128)(2,1)}, u32[]{:S(2)}) copy-start(bf16[256,1024]{1,0:T(8,128)(2,1)} %param.13) | copy-start | bytes 1572868
  7.2 8.7 %copy-start.4 = (f32[1024]{0:T(1024)S(1)}, f32[1024]{0:T(1024)}, u32[]{:S(2)}) copy-start(f32[1024]{0:T(1024)} %param.12) | copy-start | bytes 12292
  7.2 66.6 %reduce-scatter.2.cloned.1.call-start = ((), (), s32[]{:S(2)}) async-start(), calls=%async_computation.1 | async-start | bytes 2621440 | tf_op jit(solution)/shard_map/reduce_scatter | solution.py:59
  8.0 6.6 %collective-permute-start = (bf16[3,1024]{1,0:T(4,128)(2,1)S(1)}, bf16[3,1024]{1,0:T(4,128)(2,1)S(1)}, u32[]{:S(2)}, u32[]{:S(2)}) collective-permute-start(bf16[3,1024]{1,0:T(4,128)(2,1)S(1)} %get-tuple-element.14), channel_id=1, source_target_pairs={{0,4},{4,8},{8,12},{12,16},{16,20},{20,24},{24,28},{1,5},{5,9},{9,... | collective-permute-start | bytes 18440 | tf_op jit(solution)/shard_map/ppermute | solution.py:10
  10.4 6.7 %collective-permute-start.2 = (bf16[3,1024]{1,0:T(4,128)(2,1)S(1)}, bf16[3,1024]{1,0:T(4,128)(2,1)S(1)}, u32[]{:S(2)}, u32[]{:S(2)}) collective-permute-start(bf16[3,1024]{1,0:T(4,128)(2,1)S(1)} %get-tuple-element.15), channel_id=1, source_target_pairs={{4,0},{8,4},{12,8},{16,12},{20,16},{24,20},{28,24},{5,1},{9,5},{13... | collective-permute-start | bytes 18440 | tf_op jit(solution)/shard_map/ppermute | solution.py:10
  12.5 5.8 %collective-permute-start.1 = (bf16[3,1024]{1,0:T(4,128)(2,1)S(1)}, bf16[3,1024]{1,0:T(4,128)(2,1)S(1)}, u32[]{:S(2)}, u32[]{:S(2)}) collective-permute-start(bf16[3,1024]{1,0:T(4,128)(2,1)S(1)} %slice.76), channel_id=1, source_target_pairs={{4,0},{8,4},{12,8},{16,12},{20,16},{24,20},{28,24},{5,1},{9,5},{13... | collective-permute-start | bytes 18440 | tf_op jit(solution)/shard_map/ppermute | solution.py:10
  25.6 1.0 copy-start
  25.6 48.1 %copy-start.3 = (f32[4096]{0:T(1024)S(1)}, f32[4096]{0:T(1024)}, u32[]{:S(2)}) copy-start(f32[4096]{0:T(1024)} %param.8) | copy-start | bytes 49156
  73.7 41.1 %copy-start.1 = (bf16[64,4096]{1,0:T(8,128)(2,1)S(1)}, bf16[64,4096]{1,0:T(8,128)(2,1)}, u32[]{:S(2)}) copy-start(bf16[64,4096]{1,0:T(8,128)(2,1)} %reduce-scatter.2.cloned.1.call-done) | copy-start | bytes 1572868
Sparse Core Ops, SparseCore 0:
  25.8 47.9 reduce-scatter.1
where the time goes:
time: 123 us
  blocking collectives  68.9 us (56%)
  waiting for transfers between devices  18.5 us (15%)
  between operations  14.1 us (11%)
  matrix products  7.36 us (6%)
  other arithmetic  5.41 us (4%)
  starting transfers between devices  5.01 us (4%)
  local copies, waits for them, and re-layouts  3.44 us (3%)
    psum x1, blocking collectives, on_device(): lax.psum(jnp.sum(normalized_gradient * normalized_input, 0), ('ctx', 'tp'))  39.5 us
    psum x1, blocking collectives, on_device(): taps_grad, bias_grad = lax.psum((taps_part, bias_part), 'ctx')  29.4 us
    reduce_scatter x1, waiting for transfers between devices, on_device(): lax.psum_scatter(whole_term.astype(jnp.bfloat16), 'tp', scatter_dimension...  17.4 us
    dot_general x1, matrix products, on_device(): lax.dot_general(in_grad, proj_weight, (((1,), (1,)), ((), ())), preferred...  7.36 us
    ppermute x3, starting transfers between devices, from_behind(): return lax.ppermute(block, axis, route)  4.97 us
  transfers between devices with their start and end apart: 4, of which 2 were waited for; matrix products, arithmetic and copies ran while one was open for 4% of the time, Pallas kernels for 0%

commit v1 on v0

--- a/solution.py
+++ b/solution.py
@@ -62,7 +62,9 @@
     hidden_state = hidden_in.astype(jnp.float32)
     root_mean_square = jnp.sqrt(jnp.mean(hidden_state * hidden_state, -1, keepdims=True) + 1e-05)
     normalized_input = hidden_state / root_mean_square
-    norm_gain_gradient = lax.psum(jnp.sum(normalized_gradient * normalized_input, 0), ("ctx", "tp"))
+    norm_gain_gradient = jnp.sum(
+        lax.all_gather(jnp.sum(normalized_gradient * normalized_input, 0), ("ctx", "tp")), axis=0
+    )
     scaled_gradient = norm_gain[None, :] * normalized_gradient
     mean_correction = jnp.mean(scaled_gradient * normalized_input, -1, keepdims=True)
     hidden_input_gradient = (

time: 123 us -> 155 us (1.26)
  blocking collectives: 68.9 us -> 99.8 us
    all_gather x0 -> x1, blocking collectives: none -> 70.4 us  [on_device(): lax.all_gather(jnp.sum(normalized_gradient * normalized_input, 0), ('ctx'...]
    psum x1 -> x0, blocking collectives: 39.5 us -> none  [on_device(): lax.psum(jnp.sum(normalized_gradient * normalized_input, 0), ('ctx', 'tp'))]
  transfers between devices with their start and end apart: 4 -> 4, of which waited for: 2 -> 2; matrix products, arithmetic and copies ran while one was open for 4% -> 3% of each run, Pallas kernels for 0% -> 0%
where the time goes in v1:
time: 155 us; the launch traced here: 154 us
  blocking collectives  99.8 us (64%)
  waiting for transfers between devices  18.5 us (12%)
  between operations  14.2 us (9%)
  matrix products  7.36 us (5%)
  other arithmetic  6 us (4%)
  starting transfers between devices  5.01 us (3%)
  local copies, waits for them, and re-layouts  3.53 us (2%)
    all_gather x1, blocking collectives, on_device(): lax.all_gather(jnp.sum(normalized_gradient * normalized_input, 0), ('ctx'...  70.4 us
    psum x1, blocking collectives, on_device(): taps_grad, bias_grad = lax.psum((taps_part, bias_part), 'ctx')  29.4 us
    reduce_scatter x1, waiting for transfers between devices, on_device(): lax.psum_scatter(whole_term.astype(jnp.bfloat16), 'tp', scatter_dimension...  17.4 us
    dot_general x1, matrix products, on_device(): lax.dot_general(in_grad, proj_weight, (((1,), (1,)), ((), ())), preferred...  7.36 us
    ppermute x3, starting transfers between devices, from_behind(): return lax.ppermute(block, axis, route)  4.97 us
  transfers between devices with their start and end apart: 4, of which 2 were waited for; matrix products, arithmetic and copies ran while one was open for 3% of the time, Pallas kernels for 0%

profile of v1, /device:TPU:0, one launch (start us, length us, event | category | flops | bytes accessed | tf_op | source)
XLA Modules:
  0.0 154.4 jit_solution(7776847725076292415)
XLA Ops:
  7.2 0.0 copy-start.2
  7.2 0.0 copy-start.4
  7.2 0.0 reduce-scatter.2.cloned.1.call-start
  7.2 0.8 fusion.26
  8.0 2.4 %collective-permute-start = (bf16[3,1024]{1,0:T(4,128)(2,1)S(1)}, bf16[3,1024]{1,0:T(4,128)(2,1)S(1)}, u32[]{:S(2)}, u32[]{:S(2)}) collective-permute-start(bf16[3,1024]{1,0:T(4,128)(2,1)S(1)} %get-tuple-element.14), channel_id=1, source_target_pairs={{0,4},{4,8},{8,12},{12,16},{16,20},{20,24},{24,28},{1,5},{5,9},{9,... | collective-permute-start | bytes 18440 | tf_op jit(solution)/shard_map/ppermute | solution.py:10
  10.4 1.3 collective-permute-start.2
  11.7 0.7 slice.76
  12.5 1.3 collective-permute-start.1
  13.7 0.9 fusion.27
  14.6 0.0 collective-permute-done
  14.6 1.2 maximum_convert_fusion
  15.8 0.0 copy-done.2
  15.8 0.0 copy-done.4
  15.9 1.3 multiply_reduce_fusion.3
  17.1 0.0 collective-permute-done.2
  17.2 1.1 collective-permute-done.1
  18.3 7.4 %convolution_convert_fusion = bf16[256,4096]{1,0:T(8,128)(2,1)} fusion(bf16[4096,1024]{1,0:T(8,128)(2,1)} %param.9, f32[3,1024]{1,0:T(4,128)S(1)} %add_multiply_fusion.1, f32[256,1024]{1,0:T(8,128)S(1)} %get-tuple-element.13, f32[1024]{0:T(1024)S(1)} %bitcast.17, f32[1024]{0:T(1024)S(1)} %bitcast.20, f32[1024]{0:T(1024)S(1)} %bitcast.14, f32[1024]{0:T(1024)S(1)} %bitcast.11), kind=kOutput, calls=%fused_computation | convolution fusion | flops 2151415808 | bytes 11563008 | tf_op jit(solution)/shard_map/dot_general | solution.py:56
  25.6 0.0 copy-start
  25.6 0.0 copy-start.3
  25.6 0.0 reduce-scatter.2.cloned.1.call-update
  25.7 1.0 copy-done
  26.7 0.2 fusion.6
  26.9 29.4 %all-reduce = (f32[4,1024]{1,0:T(4,128)}, f32[1024]{0:T(1024)}) all-reduce(f32[4,1024]{1,0:T(4,128)S(1)} %pad_maximum_fusion.1, f32[1024]{0:T(1024)S(1)} %get-tuple-element.10), channel_id=1, replica_groups=mesh['ctx'=8,'tp'=4] {'ctx'}, use_global_device_ids=true, to_apply=%region_9.0 | all-reduce | flops 5120 | bytes 40960 | tf_op jit(solution)/shard_map/psum | solution.py:48
  56.4 17.4 %reduce-scatter.2.cloned.1.call-done = bf16[64,4096]{1,0:T(8,128)(2,1)} async-done(((bf16[256,4096]{1,0:T(8,128)(2,1)}), bf16[64,4096]{1,0:T(8,128)(2,1)}) %reduce-scatter.2.cloned.1.call-update) | async-done | bytes 524304 | tf_op jit(solution)/shard_map/reduce_scatter | solution.py:59
  73.7 0.0 copy-done.3
  73.7 1.5 fusion.5
  75.2 0.0 copy-start.1
  75.3 70.4 %all-gather = f32[131072]{0:T(1024)S(1)} all-gather(f32[4096]{0:T(1024)S(1)} %get-tuple-element.8), channel_id=2, replica_groups=mesh['ctx'=8,'tp'=4] {'ctx','tp'}, dimensions={0}, use_global_device_ids=true | all-gather | bytes 540672 | tf_op jit(solution)/shard_map/all_gather | solution.py:66
  145.7 0.1 reshape.22
  145.8 0.7 reduce_sum.84
  146.5 0.0 copy-done.1
  146.5 1.1 fusion.4
  (5 shorter events, 0.1 us)
Async XLA Ops:
  7.2 8.7 %copy-start.2 = (bf16[256,1024]{1,0:T(8,128)(2,1)S(1)}, bf16[256,1024]{1,0:T(8,128)(2,1)}, u32[]{:S(2)}) copy-start(bf16[256,1024]{1,0:T(8,128)(2,1)} %param.13) | copy-start | bytes 1572868
  7.2 8.7 %copy-start.4 = (f32[1024]{0:T(1024)S(1)}, f32[1024]{0:T(1024)}, u32[]{:S(2)}) copy-start(f32[1024]{0:T(1024)} %param.12) | copy-start | bytes 12292
  7.2 66.6 %reduce-scatter.2.cloned.1.call-start = ((), (), s32[]{:S(2)}) async-start(), calls=%async_computation.1 | async-start | bytes 2621440 | tf_op jit(solution)/shard_map/reduce_scatter | solution.py:59
  8.0 6.6 %collective-permute-start = (bf16[3,1024]{1,0:T(4,128)(2,1)S(1)}, bf16[3,1024]{1,0:T(4,128)(2,1)S(1)}, u32[]{:S(2)}, u32[]{:S(2)}) collective-permute-start(bf16[3,1024]{1,0:T(4,128)(2,1)S(1)} %get-tuple-element.14), channel_id=1, source_target_pairs={{0,4},{4,8},{8,12},{12,16},{16,20},{20,24},{24,28},{1,5},{5,9},{9,... | collective-permute-start | bytes 18440 | tf_op jit(solution)/shard_map/ppermute | solution.py:10
  10.4 6.7 %collective-permute-start.2 = (bf16[3,1024]{1,0:T(4,128)(2,1)S(1)}, bf16[3,1024]{1,0:T(4,128)(2,1)S(1)}, u32[]{:S(2)}, u32[]{:S(2)}) collective-permute-start(bf16[3,1024]{1,0:T(4,128)(2,1)S(1)} %get-tuple-element.15), channel_id=1, source_target_pairs={{4,0},{8,4},{12,8},{16,12},{20,16},{24,20},{28,24},{5,1},{9,5},{13... | collective-permute-start | bytes 18440 | tf_op jit(solution)/shard_map/ppermute | solution.py:10
  12.5 5.8 %collective-permute-start.1 = (bf16[3,1024]{1,0:T(4,128)(2,1)S(1)}, bf16[3,1024]{1,0:T(4,128)(2,1)S(1)}, u32[]{:S(2)}, u32[]{:S(2)}) collective-permute-start(bf16[3,1024]{1,0:T(4,128)(2,1)S(1)} %slice.76), channel_id=1, source_target_pairs={{4,0},{8,4},{12,8},{16,12},{20,16},{24,20},{28,24},{5,1},{9,5},{13... | collective-permute-start | bytes 18440 | tf_op jit(solution)/shard_map/ppermute | solution.py:10
  25.6 1.0 copy-start
  25.6 48.1 %copy-start.3 = (f32[4096]{0:T(1024)S(1)}, f32[4096]{0:T(1024)}, u32[]{:S(2)}) copy-start(f32[4096]{0:T(1024)} %param.8) | copy-start | bytes 49156
  75.2 71.2 %copy-start.1 = (bf16[64,4096]{1,0:T(8,128)(2,1)S(1)}, bf16[64,4096]{1,0:T(8,128)(2,1)}, u32[]{:S(2)}) copy-start(bf16[64,4096]{1,0:T(8,128)(2,1)} %reduce-scatter.2.cloned.1.call-done) | copy-start | bytes 1572868
Sparse Core Ops, SparseCore 0:
  25.8 47.9 reduce-scatter.1
